TPU v7x, 32 devices: a whole 2x2x4 slice. The times are simulated.
32 devices in a mesh: rows: 8 (over z, x), cols: 4 (over y, core).
Axes of the slice: x: 2, y: 2, z: 4, core: 2. Of those that a mesh axis runs over, the one named last changes fastest.
Arguments:
- basis: float32 [8192, 4096], P('rows', 'cols'), may hold values from -119.66257 to 119.66257, as said below
- block: float32 [8192, 512], P('rows', 'cols'), may hold values from -1800 to 1800
Outputs:
- ortho: float32 [8192, 512], P('rows', 'cols')
- factors: float32 [4, 128, 128], P('cols')
Inputs may be any that keep to these rules, and one draw needn't show every extreme that they name: Under the inner product (sum over rows divided by 8192) the basis columns have squared norms between 0.6 and 1.9, and inner products of distinct basis columns are at most 0.05 in magnitude.
All inputs are finite; a program needn't handle non-finite values.
Results may differ from a plain program's by a relative error of at most 0.000076.
Values sent between devices are 32-bit elements; how exact they have to be, the bound alone decides.
No kernel may reach another device: no remote copies, remote signals or barrier semaphores. Data moves between devices by JAX's collectives and lax.ppermute only.
A program may use at most 64 MiB of HBM per device.

v0:
```python
import jax
import jax.numpy as jnp
from jax import lax
from jax.sharding import PartitionSpec as P

BLK = 128


def solve_block(lower_factor, vectors):
    return jax.scipy.linalg.solve_triangular(lower_factor, vectors, lower=True)


def body(basis, block):
    highest = lax.Precision.HIGHEST
    local_rows = basis.shape[0]
    inverse = 1.0 / (local_rows * lax.axis_size("rows"))
    width = block.shape[1]
    column_index = lax.axis_index("cols")

    def project(piece):
        return (
            lax.dot_general(
                basis,
                piece,
                (((0,), (0,)), ((), ())),
                precision=highest,
                preferred_element_type=jnp.float32,
            )
            * inverse
        )

    def expand(coef):
        return jnp.dot(basis, coef, precision=highest, preferred_element_type=jnp.float32)

    terms_one = project(lax.all_gather(block, "cols", axis=1, tiled=True))
    coef_one = lax.psum(terms_one, "rows")
    placed = lax.dynamic_update_slice_in_dim(
        jnp.zeros((local_rows, coef_one.shape[1]), jnp.float32), block, column_index * width, 1
    )
    first_whole = lax.psum(placed - expand(coef_one), "cols")
    terms_two = project(first_whole)
    first = lax.dynamic_slice_in_dim(first_whole, column_index * width, width, 1)
    coef_two = lax.psum(terms_two, "rows")
    second = first - lax.psum_scatter(expand(coef_two), "cols", scatter_dimension=1, tiled=True)
    blocks = width // BLK
    pieces = second.reshape(local_rows, blocks, BLK)
    gram = jnp.einsum("mbi,mbj->bij", pieces, pieces, precision=highest) * inverse
    gram = lax.psum(gram, "rows")
    lower_factor = jnp.linalg.cholesky(gram)
    solved = jax.vmap(solve_block)(lower_factor, jnp.transpose(pieces, (1, 2, 0)))
    ortho = jnp.transpose(solved, (2, 0, 1)).reshape(local_rows, width)
    return (ortho, jnp.transpose(lower_factor, (0, 2, 1)))


def solution(mesh):
    placed = (P("rows", "cols"), P("rows", "cols"))
    return jax.shard_map(
        body,
        mesh=mesh,
        in_specs=placed,
        out_specs=(P("rows", "cols"), P("cols", None, None)),
        check_vma=False,
    )
```

profile of v0, /device:TPU:0, one launch (start us, length us, event | category | flops | bytes accessed | tf_op | source)
XLA Modules:
  0.0 476.0 jit_solution(7517272405939530119)
XLA Ops:
  7.2 0.0 all-gather.2.cloned.1.call-start
  7.2 0.7 all-gather.2.cloned.1.call-update
  7.9 0.0 all-reduce.5.cloned.1.call-start
  7.9 27.2 %all-gather.2.cloned.1.call-done = f32[1024,512]{1,0:T(8,128)} async-done(((f32[1024,128]{1,0:T(8,128)}), f32[1024,512]{1,0:T(8,128)}) %all-gather.2.cloned.1.call-update) | async-done | bytes 2097168 | tf_op jit(solution)/shard_map/all_gather | solution.py:35
  35.1 10.2 %convolution_multiply_fusion = f32[1024,512]{1,0:T(8,128)} fusion(f32[1024,1024]{1,0:T(8,128)} %param.2, f32[1024,512]{1,0:T(8,128)} %all-gather.2.cloned.1.call-done), kind=kOutput, calls=%fused_computation.3 | convolution fusion | flops 6442975232 | bytes 8388608 | tf_op jit(solution)/shard_map/dot_general | solution.py:22
  45.3 0.0 copy-start.1
  45.3 0.0 all-reduce.5.cloned.1.call-update
  45.3 0.0 all-reduce.7.cloned.1.call-start
  45.4 1.0 copy-done.1
  46.3 0.2 copy.4
  46.5 0.2 broadcast_in_dim.7
  46.8 0.1 constant_dynamic-update-slice_fusion
  46.8 100.9 %all-reduce.5.cloned.1.call-done = f32[1024,512]{1,0:T(8,128)} async-done(((f32[1024,512]{1,0:T(8,128)}), f32[1024,512]{1,0:T(8,128)}) %all-reduce.5.cloned.1.call-update) | async-done | bytes 2097168 | tf_op jit(solution)/shard_map/psum | solution.py:36
  147.8 16.7 %bitcast_subtract_fusion = f32[1024,512]{0,1:T(8,128)} fusion(f32[1024,512]{0,1:T(8,128)S(1)} %constant_dynamic-update-slice_fusion, f32[1024,512]{1,0:T(8,128)} %all-reduce.5.cloned.1.call-done, f32[1024,1024]{1,0:T(8,128)} %param.2), kind=kOutput, calls=%fused_computation | convolution fusion | flops 6442975232 | bytes 10485760 | tf_op jit(solution)/shard_map/dot_general | solution.py:33
  164.5 0.0 all-reduce.7.cloned.1.call-update
  164.5 0.2 all-reduce.9.cloned.1.call-start
  164.7 50.6 %all-reduce.7.cloned.1.call-done = f32[1024,512]{0,1:T(8,128)} async-done(((f32[1024,512]{0,1:T(8,128)}), f32[1024,512]{0,1:T(8,128)}) %all-reduce.7.cloned.1.call-update) | async-done | bytes 2097168 | tf_op jit(solution)/shard_map/psum | solution.py:40
  215.3 10.2 %multiply_bitcast_fusion = f32[1024,512]{0,1:T(8,128)} fusion(f32[1024,512]{0,1:T(8,128)} %all-reduce.7.cloned.1.call-done, f32[1024,1024]{1,0:T(8,128)} %param.2), kind=kOutput, calls=%fused_computation.1 | convolution fusion | flops 6442975232 | bytes 8388608 | tf_op jit(solution)/shard_map/dot_general | solution.py:22
  225.6 0.0 all-reduce.9.cloned.1.call-update
  225.6 0.0 reduce-scatter.2.cloned.1.call-start
  225.6 102.5 %all-reduce.9.cloned.1.call-done = f32[1024,512]{0,1:T(8,128)} async-done(((f32[1024,512]{0,1:T(8,128)}), f32[1024,512]{0,1:T(8,128)}) %all-reduce.9.cloned.1.call-update) | async-done | bytes 2097168 | tf_op jit(solution)/shard_map/psum | solution.py:43
  328.1 10.3 %convolution_bitcast_fusion = f32[1024,512]{0,1:T(8,128)} fusion(f32[1024,512]{0,1:T(8,128)} %all-reduce.9.cloned.1.call-done, f32[1024,1024]{1,0:T(8,128)} %param.2), kind=kOutput, calls=%fused_computation.2 | convolution fusion | flops 6442450944 | bytes 8388608 | tf_op jit(solution)/shard_map/dot_general | solution.py:33
  338.4 0.0 copy-start
  338.4 0.0 reduce-scatter.2.cloned.1.call-update
  338.4 0.3 all-reduce.11.cloned.1.call-start
  338.7 30.3 %reduce-scatter.2.cloned.1.call-done = f32[1024,128]{0,1:T(8,128)} async-done(((f32[1024,512]{0,1:T(8,128)}), f32[1024,128]{0,1:T(8,128)}) %reduce-scatter.2.cloned.1.call-update) | async-done | bytes 524304 | tf_op jit(solution)/shard_map/reduce_scatter | solution.py:44
  369.0 0.0 copy-done
  369.0 0.0 copy-start.2
  369.0 2.5 fusion
  371.5 0.0 all-reduce.11.cloned.1.call-update
  371.5 70.6 %all-reduce.11.cloned.1.call-done = f32[1,128,128]{1,2,0:T(8,128)} async-done(((f32[1,128,128]{1,2,0:T(8,128)}), f32[1,128,128]{1,2,0:T(8,128)}) %all-reduce.11.cloned.1.call-update) | async-done | bytes 65552 | tf_op jit(solution)/shard_map/psum | solution.py:48
  442.2 0.9 copy.6
  443.1 0.9 fusion.3
  444.0 11.7 %custom-call.8 = f32[1,128,128]{2,1,0:T(8,128)S(1)} custom-call(f32[1,128,128]{2,1,0:T(8,128)S(1)} %fusion.3), custom_call_target="Cholesky" | custom-call | tf_op jit(solution)/shard_map/jit(cholesky)/cholesky | solution.py:49
  455.7 0.6 compare_reduce_fusion
  456.4 0.7 fusion.4
  457.0 9.8 %custom-call.9 = f32[1,1,128,128]{2,3,1,0:T(8,128)S(1)} custom-call(f32[1,1,128,128]{3,2,1,0:T(8,128)S(1)} %get-tuple-element.5), custom_call_target="InvertDiagBlocksLowerTriangular" | custom-call | tf_op jit(solution)/shard_map/vmap(jit(_solve_triangular))/triangular_solve | solution.py:10
  466.8 0.0 copy-done.2
  466.8 0.6 convolution_bitcast_fusion.1
  467.5 1.0 copy.7
  468.5 0.7 copy.8
  (1 shorter events, 0.0 us)
Async XLA Ops:
  7.2 27.9 %all-gather.2.cloned.1.call-start = ((), (), s32[]{:S(2)}) async-start(), calls=%async_computation.1 | async-start | bytes 2621440 | tf_op jit(solution)/shard_map/all_gather | solution.py:35
  7.9 139.9 %all-reduce.5.cloned.1.call-start = ((), (), s32[]{:S(2)}) async-start(), calls=%async_computation.2 | async-start | bytes 4194304 | tf_op jit(solution)/shard_map/psum | solution.py:36
  45.3 1.0 copy-start.1
  45.3 170.0 %all-reduce.7.cloned.1.call-start = ((), (), s32[]{:S(2)}) async-start(), calls=%async_computation.3 | async-start | bytes 4194304 | tf_op jit(solution)/shard_map/psum | solution.py:40
  164.5 163.6 %all-reduce.9.cloned.1.call-start = ((), (), s32[]{:S(2)}) async-start(), calls=%async_computation.4 | async-start | bytes 4194304 | tf_op jit(solution)/shard_map/psum | solution.py:43
  225.6 143.4 %reduce-scatter.2.cloned.1.call-start = ((), (), s32[]{:S(2)}) async-start(), calls=%async_computation.5 | async-start | bytes 2621440 | tf_op jit(solution)/shard_map/reduce_scatter | solution.py:44
  338.4 30.6 %copy-start = (f32[1024,512]{0,1:T(8,128)S(1)}, f32[1024,512]{0,1:T(8,128)}, u32[]{:S(2)}) copy-start(f32[1024,512]{0,1:T(8,128)} %all-reduce.7.cloned.1.call-done) | copy-start | bytes 6291460
  338.4 103.8 %all-reduce.11.cloned.1.call-start = ((), (), s32[]{:S(2)}) async-start(), calls=%async_computation.6 | async-start | bytes 131072 | tf_op jit(solution)/shard_map/psum | solution.py:48
  369.0 97.8 %copy-start.2 = (f32[1024,128]{0,1:T(8,128)S(1)}, f32[1024,128]{0,1:T(8,128)}, u32[]{:S(2)}) copy-start(f32[1024,128]{0,1:T(8,128)} %reduce-scatter.2.cloned.1.call-done) | copy-start | bytes 1572868
Sparse Core Ops, SparseCore 0:
  9.5 25.5 all-gather.1
  45.4 102.3 all-reduce.4
  164.6 50.6 all-reduce.6
  225.7 102.3 all-reduce.8
  338.5 30.4 reduce-scatter.1
  372.9 69.2 all-reduce.10
where the time goes:
time: 476 us
  waiting for transfers between devices  383 us (80%)
  matrix products  50.5 us (11%)
  other arithmetic  23.7 us (5%)
  between operations  14.2 us (3%)
    psum x1, waiting for transfers between devices, body(): coef_two = lax.psum(terms_two, 'rows')  102 us
    psum x1, waiting for transfers between devices, body(): coef_one = lax.psum(terms_one, 'rows')  101 us
    psum x1, waiting for transfers between devices, body(): gram = lax.psum(gram, 'rows')  70.6 us
    psum x1, waiting for transfers between devices, body(): first_whole = lax.psum(placed - expand(coef_one), 'cols')  50.6 us
    reduce_scatter x1, waiting for transfers between devices, body(): lax.psum_scatter(expand(coef_two), 'cols', scatter_dimension=1, tiled=True)  30.3 us
    all_gather x1, waiting for transfers between devices, body(): terms_one = project(lax.all_gather(block, 'cols', axis=1, tiled=True))  27.2 us
    dot_general x2, matrix products, expand(): jnp.dot(basis, coef, precision=highest, preferred_element_type=jnp.float32)  27 us
    dot_general x2, matrix products, project(): lax.dot_general(basis, piece, (((0,), (0,)), ((), ())), precision=highest...  20.4 us
  transfers between devices with their start and end apart: 6, of which 6 were waited for; matrix products, arithmetic and copies ran while one was open for 0% of the time, Pallas kernels for 0%

commit v1 on v0

--- a/solution.py
+++ b/solution.py
@@ -4,6 +4,11 @@
 from jax.sharding import PartitionSpec as P
 
 BLK = 128
+
+
+def gather_and_add(shard, axis):
+    pieces = lax.all_gather(shard, axis)
+    return jnp.sum(pieces, axis=0)
 
 
 def solve_block(lower_factor, vectors):
@@ -45,7 +50,7 @@
     blocks = width // BLK
     pieces = second.reshape(local_rows, blocks, BLK)
     gram = jnp.einsum("mbi,mbj->bij", pieces, pieces, precision=highest) * inverse
-    gram = lax.psum(gram, "rows")
+    gram = gather_and_add(gram, "rows")
     lower_factor = jnp.linalg.cholesky(gram)
     solved = jax.vmap(solve_block)(lower_factor, jnp.transpose(pieces, (1, 2, 0)))
     ortho = jnp.transpose(solved, (2, 0, 1)).reshape(local_rows, width)

time: 476 us -> 435 us (0.914)
  waiting for transfers between devices: 383 us -> 312 us
  blocking collectives: 0 us -> 31.8 us
    psum x1 -> x0, waiting for transfers between devices: 70.6 us -> none  [body(): gram = lax.psum(gram, 'rows')]
    all_gather x0 -> x1, blocking collectives: none -> 31.8 us  [gather_and_add(): pieces = lax.all_gather(shard, axis)]
  transfers between devices with their start and end apart: 6 -> 5, of which waited for: 6 -> 5; matrix products, arithmetic and copies ran while one was open for 0% -> 0% of each run, Pallas kernels for 0% -> 0%
where the time goes in v1:
time: 435 us
  waiting for transfers between devices  312 us (72%)
  matrix products  49.9 us (11%)
  blocking collectives  31.8 us (7%)
  other arithmetic  22.9 us (5%)
  between operations  13.9 us (3%)
    psum x1, waiting for transfers between devices, body(): coef_two = lax.psum(terms_two, 'rows')  102 us
    psum x1, waiting for transfers between devices, body(): coef_one = lax.psum(terms_one, 'rows')  101 us
    psum x1, waiting for transfers between devices, body(): first_whole = lax.psum(placed - expand(coef_one), 'cols')  50.6 us
    all_gather x1, blocking collectives, gather_and_add(): pieces = lax.all_gather(shard, axis)  31.8 us
    reduce_scatter x1, waiting for transfers between devices, body(): lax.psum_scatter(expand(coef_two), 'cols', scatter_dimension=1, tiled=True)  30.6 us
    all_gather x1, waiting for transfers between devices, body(): terms_one = project(lax.all_gather(block, 'cols', axis=1, tiled=True))  27.2 us
    dot_general x2, matrix products, expand(): jnp.dot(basis, coef, precision=highest, preferred_element_type=jnp.float32)  27 us
    dot_general x2, matrix products, project(): lax.dot_general(basis, piece, (((0,), (0,)), ((), ())), precision=highest...  20.4 us
  transfers between devices with their start and end apart: 5, of which 5 were waited for; matrix products, arithmetic and copies ran while one was open for 0% of the time, Pallas kernels for 0%

profile of v1, /device:TPU:0, one launch (start us, length us, event | category | flops | bytes accessed | tf_op | source)
XLA Modules:
  0.0 434.7 jit_solution(803231580015927333)
XLA Ops:
  7.2 0.0 all-gather.3.cloned.1.call-start
  7.2 0.7 all-gather.3.cloned.1.call-update
  7.9 0.0 all-reduce.4.cloned.1.call-start
  7.9 27.2 %all-gather.3.cloned.1.call-done = f32[1024,512]{1,0:T(8,128)} async-done(((f32[1024,128]{1,0:T(8,128)}), f32[1024,512]{1,0:T(8,128)}) %all-gather.3.cloned.1.call-update) | async-done | bytes 2097168 | tf_op jit(solution)/shard_map/all_gather | solution.py:40
  35.1 10.2 %convolution_multiply_fusion = f32[1024,512]{1,0:T(8,128)} fusion(f32[1024,1024]{1,0:T(8,128)} %param.2, f32[1024,512]{1,0:T(8,128)} %all-gather.3.cloned.1.call-done), kind=kOutput, calls=%fused_computation.3 | convolution fusion | flops 6442975232 | bytes 8388608 | tf_op jit(solution)/shard_map/dot_general | solution.py:27
  45.3 0.0 copy-start.1
  45.3 0.0 all-reduce.4.cloned.1.call-update
  45.3 0.0 all-reduce.6.cloned.1.call-start
  45.4 1.0 copy-done.1
  46.3 0.2 copy.8
  46.5 0.2 broadcast_in_dim.7
  46.8 0.1 constant_dynamic-update-slice_fusion
  46.9 100.9 %all-reduce.4.cloned.1.call-done = f32[1024,512]{1,0:T(8,128)} async-done(((f32[1024,512]{1,0:T(8,128)}), f32[1024,512]{1,0:T(8,128)}) %all-reduce.4.cloned.1.call-update) | async-done | bytes 2097168 | tf_op jit(solution)/shard_map/psum | solution.py:41
  147.8 16.7 %bitcast_subtract_fusion = f32[1024,512]{0,1:T(8,128)} fusion(f32[1024,512]{0,1:T(8,128)S(1)} %constant_dynamic-update-slice_fusion, f32[1024,512]{1,0:T(8,128)} %all-reduce.4.cloned.1.call-done, f32[1024,1024]{1,0:T(8,128)} %param.2), kind=kOutput, calls=%fused_computation | convolution fusion | flops 6442975232 | bytes 10485760 | tf_op jit(solution)/shard_map/dot_general | solution.py:38
  164.4 0.0 all-reduce.6.cloned.1.call-update
  164.5 0.2 all-reduce.8.cloned.1.call-start
  164.7 50.6 %all-reduce.6.cloned.1.call-done = f32[1024,512]{0,1:T(8,128)} async-done(((f32[1024,512]{0,1:T(8,128)}), f32[1024,512]{0,1:T(8,128)}) %all-reduce.6.cloned.1.call-update) | async-done | bytes 2097168 | tf_op jit(solution)/shard_map/psum | solution.py:45
  215.3 10.3 %multiply_bitcast_fusion = f32[1024,512]{0,1:T(8,128)} fusion(f32[1024,512]{0,1:T(8,128)} %all-reduce.6.cloned.1.call-done, f32[1024,1024]{1,0:T(8,128)} %param.2), kind=kOutput, calls=%fused_computation.1 | convolution fusion | flops 6442975232 | bytes 8388608 | tf_op jit(solution)/shard_map/dot_general | solution.py:27
  225.5 0.0 all-reduce.8.cloned.1.call-update
  225.6 0.0 reduce-scatter.2.cloned.1.call-start
  225.6 102.5 %all-reduce.8.cloned.1.call-done = f32[1024,512]{0,1:T(8,128)} async-done(((f32[1024,512]{0,1:T(8,128)}), f32[1024,512]{0,1:T(8,128)}) %all-reduce.8.cloned.1.call-update) | async-done | bytes 2097168 | tf_op jit(solution)/shard_map/psum | solution.py:48
  328.1 10.3 %convolution_bitcast_fusion = f32[1024,512]{0,1:T(8,128)} fusion(f32[1024,512]{0,1:T(8,128)} %all-reduce.8.cloned.1.call-done, f32[1024,1024]{1,0:T(8,128)} %param.2), kind=kOutput, calls=%fused_computation.2 | convolution fusion | flops 6442450944 | bytes 8388608 | tf_op jit(solution)/shard_map/dot_general | solution.py:38
  338.4 0.0 copy-start
  338.4 0.0 reduce-scatter.2.cloned.1.call-update
  338.4 30.6 %reduce-scatter.2.cloned.1.call-done = f32[1024,128]{0,1:T(8,128)} async-done(((f32[1024,512]{0,1:T(8,128)}), f32[1024,128]{0,1:T(8,128)}) %reduce-scatter.2.cloned.1.call-update) | async-done | bytes 524304 | tf_op jit(solution)/shard_map/reduce_scatter | solution.py:49
  369.0 0.0 copy-done
  369.0 0.0 copy-start.2
  369.0 1.9 convolution_multiply_fusion.1
  370.9 31.8 %all-gather = f32[1024,128]{1,0:T(8,128)S(1)} all-gather(f32[128,128]{1,0:T(8,128)S(1)} %convolution_multiply_fusion.1), channel_id=2, replica_groups=mesh['rows'=8,'cols'=4] {'rows'}, dimensions={0}, use_global_device_ids=true | all-gather | bytes 589824 | tf_op jit(solution)/shard_map/all_gather | solution.py:10
  402.7 0.1 copy.9
  402.8 0.1 copy.10
  402.9 11.7 %custom-call.8 = f32[1,128,128]{2,1,0:T(8,128)S(1)} custom-call(f32[1,128,128]{2,1,0:T(8,128)S(1)} %fusion.1), custom_call_target="Cholesky" | custom-call | tf_op jit(solution)/shard_map/jit(cholesky)/cholesky | solution.py:54
  414.6 0.6 compare_reduce_fusion
  415.3 0.7 fusion.3
  415.9 9.8 %custom-call.9 = f32[1,1,128,128]{2,3,1,0:T(8,128)S(1)} custom-call(f32[1,1,128,128]{3,2,1,0:T(8,128)S(1)} %get-tuple-element.7), custom_call_target="InvertDiagBlocksLowerTriangular" | custom-call | tf_op jit(solution)/shard_map/vmap(jit(_solve_triangular))/triangular_solve | solution.py:15
  425.8 0.0 copy-done.2
  425.8 0.6 convolution_bitcast_fusion.1
  426.4 1.0 copy.11
  427.4 0.7 copy.12
  (3 shorter events, 0.1 us)
Async XLA Ops:
  7.2 27.9 %all-gather.3.cloned.1.call-start = ((), (), s32[]{:S(2)}) async-start(), calls=%async_computation.1 | async-start | bytes 2621440 | tf_op jit(solution)/shard_map/all_gather | solution.py:40
  7.9 139.9 %all-reduce.4.cloned.1.call-start = ((), (), s32[]{:S(2)}) async-start(), calls=%async_computation.2 | async-start | bytes 4194304 | tf_op jit(solution)/shard_map/psum | solution.py:41
  45.3 1.0 copy-start.1
  45.3 170.0 %all-reduce.6.cloned.1.call-start = ((), (), s32[]{:S(2)}) async-start(), calls=%async_computation.3 | async-start | bytes 4194304 | tf_op jit(solution)/shard_map/psum | solution.py:45
  164.5 163.6 %all-reduce.8.cloned.1.call-start = ((), (), s32[]{:S(2)}) async-start(), calls=%async_computation.4 | async-start | bytes 4194304 | tf_op jit(solution)/shard_map/psum | solution.py:48
  225.6 143.4 %reduce-scatter.2.cloned.1.call-start = ((), (), s32[]{:S(2)}) async-start(), calls=%async_computation.5 | async-start | bytes 2621440 | tf_op jit(solution)/shard_map/reduce_scatter | solution.py:49
  338.4 30.6 %copy-start = (f32[1024,512]{0,1:T(8,128)S(1)}, f32[1024,512]{0,1:T(8,128)}, u32[]{:S(2)}) copy-start(f32[1024,512]{0,1:T(8,128)} %all-reduce.6.cloned.1.call-done) | copy-start | bytes 6291460
  369.0 56.8 %copy-start.2 = (f32[1024,128]{0,1:T(8,128)S(1)}, f32[1024,128]{0,1:T(8,128)}, u32[]{:S(2)}) copy-start(f32[1024,128]{0,1:T(8,128)} %reduce-scatter.2.cloned.1.call-done) | copy-start | bytes 1572868
Sparse Core Ops, SparseCore 0:
  9.5 25.5 all-gather.2
  45.4 102.2 all-reduce.3
  164.6 50.6 all-reduce.5
  225.7 102.3 all-reduce.7
  338.5 30.4 reduce-scatter.1
